TPU v7x, 128 devices: a whole 4x4x4 slice. The times are simulated.
128 devices in a mesh: layer: 2 (over core), expert: 16 (over y, x), matrix: 4 (over z).
Axes of the slice: x: 4, y: 4, z: 4, core: 2. Of those that a mesh axis runs over, the one named last changes fastest.
Arguments:
- grads: float32 [32, 1, 2048, 768], P(('layer', 'expert'), None, 'matrix'), parts along dimension 0, may hold values from -6 to 6
- basis_out: float32 [32, 2048, 2048], P('layer', None, ('expert', 'matrix')), parts along dimension 0, may hold values from -0.125 to 0.125
- basis_in: float32 [32, 768, 768], P('layer', ('expert', 'matrix')), parts along dimension 0, may hold values from -0.21875 to 0.21875
- eigvals: float32 [32, 2048, 768], P('layer', ('expert', 'matrix')), parts along dimension 0, may hold values from 0.001 to 1
- counts: int32 [32], P(('layer', 'expert')), parts along dimension 0, may hold values from 0 to 1, as said below
- slot_query: int32 [32, 1], P(('layer', 'expert')), parts along dimension 0, may hold values from 0 to 31
Outputs:
- precond: float32 [32, 1, 2048, 768], P(('layer', 'expert'), None, 'matrix'), parts along dimension 0
- scores: float32 [64], P('layer'), parts along dimension 0
There are 2 independent parts, one for each index of `layer`. A program takes and returns all parts, laid end to end along the dimension named above; each array names one. Nothing has to cross between parts.
Inputs may be any that keep to these rules, and one draw needn't show every extreme that they name: `counts`: some expert has no live slot and some expert has all 1.
All inputs are finite; a program needn't handle non-finite values.
Results may differ from a plain program's by a relative error of at most 0.0003.
Values sent between devices are 32-bit elements; how exact they have to be, the bound alone decides.
A program may use at most 64 MiB of HBM per device.

v0:
```python
import jax
import jax.numpy as jnp
from jax import lax
from jax.sharding import PartitionSpec as P

QUERIES = 32
damping_fixed = 0.05
highest = lax.Precision.HIGHEST


def shards(grads, basis_out, basis_in, eigvals, counts, slot_query):
    capacity = grads.shape[1]
    own_rows = grads.shape[2]
    in_width = grads.shape[3]
    groups = lax.axis_size("matrix")
    columns = lax.all_to_all(basis_out, "expert", split_axis=0, concat_axis=2, tiled=True)[0]
    scales, inner = (
        lax.all_to_all(eigvals, "expert", split_axis=0, concat_axis=1, tiled=True),
        lax.all_to_all(basis_in, "expert", split_axis=0, concat_axis=1, tiled=True),
    )
    inner = lax.all_gather(inner, "matrix", axis=1, tiled=True)[0]
    sources = lax.axis_size("expert")
    inner = inner.reshape(groups, sources, -1, in_width).transpose(1, 0, 2, 3).reshape(-1, in_width)
    divisor = scales[0] + damping_fixed
    live_count = counts[0]
    queries = slot_query[0]
    local_rows = grads[0]
    slot_ids = jnp.arange(capacity, dtype=jnp.int32)
    live = (slot_ids < live_count).astype(jnp.float32)
    rotated = jnp.einsum(
        "ik,if->kf",
        columns,
        lax.all_gather(local_rows[0], "matrix", axis=0, tiled=True),
        precision=highest,
    )
    rotated = jnp.dot(rotated, inner, precision=highest)
    scaled = rotated / divisor
    back = jnp.einsum("kg,hg->kh", scaled, inner, precision=highest)

    def project_one(start, amount, back=back):
        return jnp.dot(columns, back, precision=highest)

    result = lax.psum_scatter(
        project_one(jnp.int32(0), own_rows * lax.axis_size("matrix")),
        "matrix",
        scatter_dimension=0,
        tiled=True,
    )
    results = [result * live[0]]
    precond = jnp.stack(results)
    values = jnp.sum(local_rows * precond, axis=(1, 2)) / (own_rows * groups * in_width)
    targets = jnp.arange(QUERIES, dtype=jnp.int32)
    onehot = (queries[:, None] == targets[None, :]).astype(jnp.float32)
    partial_scores = jnp.sum(values[:, None] * onehot, axis=0)
    scores = lax.psum(partial_scores, ("expert", "matrix"))
    return (precond[None], scores)


def solution(mesh):
    in_specs = (
        P(("layer", "expert"), None, "matrix", None),
        P("layer", None, ("expert", "matrix")),
        P("layer", ("expert", "matrix"), None),
        P("layer", ("expert", "matrix"), None),
        P(("layer", "expert")),
        P(("layer", "expert"), None),
    )
    out_specs = (P(("layer", "expert"), None, "matrix", None), P("layer"))
    return jax.shard_map(shards, mesh=mesh, in_specs=in_specs, out_specs=out_specs, check_vma=False)
```

profile of v0, /device:TPU:0, one launch (start us, length us, event | category | flops | bytes accessed | tf_op | source)
XLA Modules:
  0.0 419.3 jit_solution(11684869709950085901)
XLA Ops:
  7.2 0.0 all-gather.4.cloned.1.call-start
  7.2 1.4 copy.14
  8.6 21.3 %all_to_all.36 = f32[16,12,768]{2,1,0:T(8,128)S(1)} all-to-all(f32[16,12,768]{2,1,0:T(8,128)S(1)} %copy.14), channel_id=1, replica_groups=mesh['layer'=2,'expert'=16,'matrix'=4] {'expert'}, dimensions={0} | all-to-all | bytes 1179648 | tf_op jit(solution)/shard_map/all_to_all | solution.py:19
  29.9 0.0 copy-start.2
  29.9 0.9 all_to_all.31
  30.9 0.0 all-gather.4.cloned.1.call-update
  30.9 0.0 all-gather.6.cloned.1.call-start
  30.9 0.7 all-gather.6.cloned.1.call-update
  31.6 0.0 copy-done.2
  31.6 25.2 %all_to_all.37 = f32[16,32,768]{2,1,0:T(8,128)S(1)} all-to-all(f32[16,32,768]{2,1,0:T(8,128)S(1)} %copy-done.2), channel_id=1, replica_groups=mesh['layer'=2,'expert'=16,'matrix'=4] {'expert'}, dimensions={0} | all-to-all | bytes 3145728 | tf_op jit(solution)/shard_map/all_to_all | solution.py:18
  56.8 4.5 %all-to-all-start = ((f32[16,2048,32]{1,2,0:T(8,128)}), f32[16,2048,32]{1,2,0:T(8,128)}, u32[]{:S(2)}, u32[]{:S(2)}) async-start(f32[16,2048,32]{1,2,0:T(8,128)} %param.7), calls=%async_computation | async-start | bytes 8388608 | tf_op jit(solution)/shard_map/all_to_all | solution.py:16
  61.3 0.0 reduce-scatter.2.cloned.1.call-start
  61.4 1.3 broadcast_add_fusion
  62.7 0.0 all-gather.4.cloned.1.call-done
  62.7 2.4 reshape_squeeze.3
  65.1 2.0 copy.15
  67.2 2.6 reshape.33
  69.8 51.2 %all-to-all-done = f32[16,2048,32]{1,2,0:T(8,128)} async-done(((f32[16,2048,32]{1,2,0:T(8,128)}), f32[16,2048,32]{1,2,0:T(8,128)}, u32[]{:S(2)}, u32[]{:S(2)}) %all-to-all-start) | async-done | bytes 4194336 | tf_op jit(solution)/shard_map/all_to_all | solution.py:16
  121.0 9.2 %all-gather.6.cloned.1.call-done = f32[1,1,2048,768]{3,2,1,0:T(8,128)} async-done(((f32[1,1,512,768]{3,2,1,0:T(8,128)}), f32[1,1,2048,768]{3,2,1,0:T(8,128)}) %all-gather.6.cloned.1.call-update) | async-done | bytes 6291472 | tf_op jit(solution)/shard_map/all_gather | solution.py:33
  130.1 0.0 copy-start.1
  130.1 13.4 %fusion = f32[512,768]{1,0:T(8,128)S(1)} fusion(f32[2048,512]{0,1:T(8,128)} %bitcast.2, f32[1,1,2048,768]{3,2,1,0:T(8,128)} %all-gather.6.cloned.1.call-done), kind=kOutput, calls=%fused_computation | convolution fusion | flops 9663676416 | bytes 12058624 | tf_op jit(solution)/shard_map/ik,if->kf/dot_general | solution.py:30
  143.5 0.0 copy-done.1
  143.5 4.1 bitcast_divide_fusion
  147.6 4.0 fusion.3
  151.6 14.2 %convolution_bitcast_fusion = f32[2048,768]{0,1:T(8,128)} fusion(f32[512,768]{1,0:T(8,128)S(1)} %fusion.3, f32[2048,512]{0,1:T(8,128)} %bitcast.2), kind=kOutput, calls=%fused_computation.2 | convolution fusion | flops 9663676416 | bytes 12058624 | tf_op jit(solution)/shard_map/dot_general | solution.py:41
  165.8 0.0 copy-start
  165.8 0.0 reduce-scatter.2.cloned.1.call-update
  165.8 1.4 copy-done
  167.2 0.5 copy.16
  168.9 61.7 %reduce-scatter.2.cloned.1.call-done = f32[512,768]{0,1:T(8,128)} async-done(((f32[2048,768]{0,1:T(8,128)}), f32[512,768]{0,1:T(8,128)}) %reduce-scatter.2.cloned.1.call-update) | async-done | bytes 1572880 | tf_op jit(solution)/shard_map/reduce_scatter | solution.py:43
  230.6 2.5 fusion.2
  233.1 1.6 copy.17
  235.5 177.3 %psum.7 = f32[32]{0:T(128)} all-reduce(f32[32]{0:T(128)S(1)} %compare_select_fusion), channel_id=1, replica_groups=mesh['layer'=2,'expert'=16,'matrix'=4] {'expert','matrix'}, use_global_device_ids=true, to_apply=%region_2.0 | all-reduce | flops 32 | bytes 256 | tf_op jit(solution)/shard_map/psum | solution.py:55
  (1 shorter events, 0.0 us)
Async XLA Ops:
  7.2 55.5 %all-gather.4.cloned.1.call-start = ((), (), s32[]{:S(2)}) async-start(), calls=%async_computation.4 | async-start | bytes 2949120 | tf_op jit(solution)/shard_map/all_gather | solution.py:21
  29.9 1.7 copy-start.2
  30.9 99.2 %all-gather.6.cloned.1.call-start = ((), (), s32[]{:S(2)}) async-start(), calls=%async_computation.6 | async-start | bytes 7864320 | tf_op jit(solution)/shard_map/all_gather | solution.py:33
  56.8 64.2 %all-to-all-start = ((f32[16,2048,32]{1,2,0:T(8,128)}), f32[16,2048,32]{1,2,0:T(8,128)}, u32[]{:S(2)}, u32[]{:S(2)}) async-start(f32[16,2048,32]{1,2,0:T(8,128)} %param.7), calls=%async_computation | async-start | bytes 8388608 | tf_op jit(solution)/shard_map/all_to_all | solution.py:16
  61.3 169.3 %reduce-scatter.2.cloned.1.call-start = ((), (), s32[]{:S(2)}) async-start(), calls=%async_computation.5 | async-start | bytes 7864320 | tf_op jit(solution)/shard_map/reduce_scatter | solution.py:43
  130.1 13.4 %copy-start.1 = (f32[16,32,768]{2,1,0:T(8,128)S(1)}, f32[16,32,768]{2,1,0:T(8,128)}, u32[]{:S(2)}) copy-start(f32[16,32,768]{2,1,0:T(8,128)} %broadcast_add_fusion) | copy-start | bytes 4718596
  165.8 1.4 copy-start
Sparse Core Ops, SparseCore 0:
  31.0 31.6 all-gather.3
  64.3 65.7 all-gather.5
  165.9 64.6 reduce-scatter.1
where the time goes:
time: 420 us; the launch traced here: 419 us
  blocking collectives  224 us (53%)
  waiting for transfers between devices  123 us (29%)
  matrix products  35.6 us (8%)
  between operations  15.8 us (4%)
  local copies, waits for them, and re-layouts  12.9 us (3%)
  starting transfers between devices  4.66 us (1%)
    psum x1, blocking collectives, shards(): scores = lax.psum(partial_scores, ('expert', 'matrix'))  177 us
    reduce_scatter x1, waiting for transfers between devices, shards(): lax.psum_scatter(project_one(jnp.int32(0), own_rows * lax.axis_size('matr...  61.7 us
    all_to_all x1, waiting for transfers between devices, shards(): lax.all_to_all(basis_out, 'expert', split_axis=0, concat_axis=2, tiled=True)  51.2 us
    all_to_all x1, blocking collectives, shards(): lax.all_to_all(eigvals, 'expert', split_axis=0, concat_axis=1, tiled=True)  25.2 us
    all_to_all x1, blocking collectives, shards(): lax.all_to_all(basis_in, 'expert', split_axis=0, concat_axis=1, tiled=True)  21.3 us
    dot_general x1, matrix products, project_one(): return jnp.dot(columns, back, precision=highest)  14.2 us
    dot_general x1, matrix products, shards(): jnp.einsum('ik,if->kf', columns, lax.all_gather(local_rows[0], 'matrix',...  13.4 us
    all_gather x1, waiting for transfers between devices, shards(): lax.all_gather(local_rows[0], 'matrix', axis=0, tiled=True)  9.16 us
  transfers between devices with their start and end apart: 4, of which 3 were waited for; matrix products, arithmetic and copies ran while one was open for 2% of the time, Pallas kernels for 0%

commit v1 on v0

--- a/solution.py
+++ b/solution.py
@@ -52,7 +52,7 @@
     targets = jnp.arange(QUERIES, dtype=jnp.int32)
     onehot = (queries[:, None] == targets[None, :]).astype(jnp.float32)
     partial_scores = jnp.sum(values[:, None] * onehot, axis=0)
-    scores = lax.psum(partial_scores, ("expert", "matrix"))
+    scores = lax.psum(lax.psum(partial_scores, "expert"), "matrix")
     return (precond[None], scores)
 
 

time: 420 us -> 292 us (0.70)
  blocking collectives: 224 us -> 95.7 us
    psum x1 -> x2, blocking collectives: 177 us -> 49.3 us  [shards(): scores = lax.psum(lax.psum(partial_scores, 'expert'), 'matrix')]
  transfers between devices with their start and end apart: 4 -> 4, of which waited for: 3 -> 3; matrix products, arithmetic and copies ran while one was open for 2% -> 3% of each run, Pallas kernels for 0% -> 0%
where the time goes in v1:
time: 292 us; the launch traced here: 291 us
  waiting for transfers between devices  123 us (42%)
  blocking collectives  95.7 us (33%)
  matrix products  35.5 us (12%)
  between operations  15.7 us (5%)
  local copies, waits for them, and re-layouts  12.9 us (4%)
  starting transfers between devices  4.67 us (2%)
  other arithmetic  3.77 us (1%)
    reduce_scatter x1, waiting for transfers between devices, shards(): lax.psum_scatter(project_one(jnp.int32(0), own_rows * lax.axis_size('matr...  61.7 us
    all_to_all x1, waiting for transfers between devices, shards(): lax.all_to_all(basis_out, 'expert', split_axis=0, concat_axis=2, tiled=True)  51.2 us
    psum x2, blocking collectives, shards(): scores = lax.psum(lax.psum(partial_scores, 'expert'), 'matrix')  49.3 us
    all_to_all x1, blocking collectives, shards(): lax.all_to_all(eigvals, 'expert', split_axis=0, concat_axis=1, tiled=True)  25.2 us
    all_to_all x1, blocking collectives, shards(): lax.all_to_all(basis_in, 'expert', split_axis=0, concat_axis=1, tiled=True)  21.3 us
    dot_general x1, matrix products, project_one(): return jnp.dot(columns, back, precision=highest)  14.1 us
    dot_general x1, matrix products, shards(): jnp.einsum('ik,if->kf', columns, lax.all_gather(local_rows[0], 'matrix',...  13.4 us
    all_gather x1, waiting for transfers between devices, shards(): lax.all_gather(local_rows[0], 'matrix', axis=0, tiled=True)  9.14 us
  transfers between devices with their start and end apart: 4, of which 3 were waited for; matrix products, arithmetic and copies ran while one was open for 3% of the time, Pallas kernels for 0%

profile of v1, /device:TPU:0, one launch (start us, length us, event | category | flops | bytes accessed | tf_op | source)
XLA Modules:
  0.0 291.1 jit_solution(15411120259842075962)
XLA Ops:
  7.2 0.0 all-gather.4.cloned.1.call-start
  7.2 1.4 copy.14
  8.6 21.3 %all_to_all.36 = f32[16,12,768]{2,1,0:T(8,128)S(1)} all-to-all(f32[16,12,768]{2,1,0:T(8,128)S(1)} %copy.14), channel_id=1, replica_groups=mesh['layer'=2,'expert'=16,'matrix'=4] {'expert'}, dimensions={0} | all-to-all | bytes 1179648 | tf_op jit(solution)/shard_map/all_to_all | solution.py:19
  29.9 0.0 copy-start.2
  29.9 0.9 all_to_all.31
  30.9 0.0 all-gather.4.cloned.1.call-update
  30.9 0.0 all-gather.6.cloned.1.call-start
  30.9 0.7 all-gather.6.cloned.1.call-update
  31.6 0.0 copy-done.2
  31.7 25.2 %all_to_all.37 = f32[16,32,768]{2,1,0:T(8,128)S(1)} all-to-all(f32[16,32,768]{2,1,0:T(8,128)S(1)} %copy-done.2), channel_id=1, replica_groups=mesh['layer'=2,'expert'=16,'matrix'=4] {'expert'}, dimensions={0} | all-to-all | bytes 3145728 | tf_op jit(solution)/shard_map/all_to_all | solution.py:18
  56.8 4.6 %all-to-all-start = ((f32[16,2048,32]{1,2,0:T(8,128)}), f32[16,2048,32]{1,2,0:T(8,128)}, u32[]{:S(2)}, u32[]{:S(2)}) async-start(f32[16,2048,32]{1,2,0:T(8,128)} %param.7), calls=%async_computation | async-start | bytes 8388608 | tf_op jit(solution)/shard_map/all_to_all | solution.py:16
  61.4 0.0 reduce-scatter.2.cloned.1.call-start
  61.4 1.3 broadcast_add_fusion
  62.7 0.0 all-gather.4.cloned.1.call-done
  62.7 2.4 reshape_squeeze.3
  65.2 2.0 copy.15
  67.2 2.6 reshape.33
  69.8 51.2 %all-to-all-done = f32[16,2048,32]{1,2,0:T(8,128)} async-done(((f32[16,2048,32]{1,2,0:T(8,128)}), f32[16,2048,32]{1,2,0:T(8,128)}, u32[]{:S(2)}, u32[]{:S(2)}) %all-to-all-start) | async-done | bytes 4194336 | tf_op jit(solution)/shard_map/all_to_all | solution.py:16
  121.0 9.1 %all-gather.6.cloned.1.call-done = f32[1,1,2048,768]{3,2,1,0:T(8,128)} async-done(((f32[1,1,512,768]{3,2,1,0:T(8,128)}), f32[1,1,2048,768]{3,2,1,0:T(8,128)}) %all-gather.6.cloned.1.call-update) | async-done | bytes 6291472 | tf_op jit(solution)/shard_map/all_gather | solution.py:33
  130.1 0.0 copy-start.1
  130.1 13.4 %fusion = f32[512,768]{1,0:T(8,128)S(1)} fusion(f32[2048,512]{0,1:T(8,128)} %bitcast.2, f32[1,1,2048,768]{3,2,1,0:T(8,128)} %all-gather.6.cloned.1.call-done), kind=kOutput, calls=%fused_computation | convolution fusion | flops 9663676416 | bytes 12058624 | tf_op jit(solution)/shard_map/ik,if->kf/dot_general | solution.py:30
  143.5 0.0 copy-done.1
  143.5 4.1 %bitcast_divide_fusion = f32[512,768]{1,0:T(8,128)S(1)} fusion(f32[16,32,768]{2,1,0:T(8,128)S(1)} %copy-done.1, f32[512,768]{1,0:T(8,128)S(1)} %fusion, f32[768,768]{1,0:T(8,128)S(1)} %reshape.33), kind=kOutput, calls=%fused_computation.5 | convolution fusion | flops 3624271872 | bytes 7077888 | tf_op jit(solution)/shard_map/dot_general | solution.py:36
  147.6 4.0 %fusion.3 = f32[512,768]{1,0:T(8,128)S(1)} fusion(f32[512,768]{1,0:T(8,128)S(1)} %bitcast_divide_fusion, f32[768,768]{1,0:T(8,128)S(1)} %reshape.33), kind=kOutput, calls=%fused_computation.9 | convolution fusion | flops 3623878656 | bytes 5505024 | tf_op jit(solution)/shard_map/kg,hg->kh/dot_general | solution.py:38
  151.6 14.1 %convolution_bitcast_fusion = f32[2048,768]{0,1:T(8,128)} fusion(f32[512,768]{1,0:T(8,128)S(1)} %fusion.3, f32[2048,512]{0,1:T(8,128)} %bitcast.2), kind=kOutput, calls=%fused_computation.2 | convolution fusion | flops 9663676416 | bytes 12058624 | tf_op jit(solution)/shard_map/dot_general | solution.py:41
  165.7 0.0 copy-start
  165.7 0.0 reduce-scatter.2.cloned.1.call-update
  165.7 1.4 copy-done
  167.1 0.5 copy.16
  168.9 61.7 %reduce-scatter.2.cloned.1.call-done = f32[512,768]{0,1:T(8,128)} async-done(((f32[2048,768]{0,1:T(8,128)}), f32[512,768]{0,1:T(8,128)}) %reduce-scatter.2.cloned.1.call-update) | async-done | bytes 1572880 | tf_op jit(solution)/shard_map/reduce_scatter | solution.py:43
  230.6 2.5 fusion.2
  233.0 1.6 copy.17
  235.3 40.3 %psum.14 = f32[32]{0:T(128)S(1)} all-reduce(f32[32]{0:T(128)S(1)} %compare_select_fusion), channel_id=1, replica_groups=mesh['layer'=2,'expert'=16,'matrix'=4] {'expert'}, use_global_device_ids=true, to_apply=%region_2.0 | all-reduce | flops 32 | bytes 256 | tf_op jit(solution)/shard_map/psum | solution.py:55
  275.6 9.0 %psum.15 = f32[32]{0:T(128)} all-reduce(f32[32]{0:T(128)S(1)} %psum.14), channel_id=1, replica_groups=mesh['layer'=2,'expert'=16,'matrix'=4] {'matrix'}, use_global_device_ids=true, to_apply=%region_3.0 | all-reduce | flops 32 | bytes 256 | tf_op jit(solution)/shard_map/psum | solution.py:55
  (1 shorter events, 0.0 us)
Async XLA Ops:
  7.2 55.6 %all-gather.4.cloned.1.call-start = ((), (), s32[]{:S(2)}) async-start(), calls=%async_computation.4 | async-start | bytes 2949120 | tf_op jit(solution)/shard_map/all_gather | solution.py:21
  29.9 1.7 copy-start.2
  30.9 99.2 %all-gather.6.cloned.1.call-start = ((), (), s32[]{:S(2)}) async-start(), calls=%async_computation.6 | async-start | bytes 7864320 | tf_op jit(solution)/shard_map/all_gather | solution.py:33
  56.8 64.2 %all-to-all-start = ((f32[16,2048,32]{1,2,0:T(8,128)}), f32[16,2048,32]{1,2,0:T(8,128)}, u32[]{:S(2)}, u32[]{:S(2)}) async-start(f32[16,2048,32]{1,2,0:T(8,128)} %param.7), calls=%async_computation | async-start | bytes 8388608 | tf_op jit(solution)/shard_map/all_to_all | solution.py:16
  61.4 169.2 %reduce-scatter.2.cloned.1.call-start = ((), (), s32[]{:S(2)}) async-start(), calls=%async_computation.5 | async-start | bytes 7864320 | tf_op jit(solution)/shard_map/reduce_scatter | solution.py:43
  130.1 13.4 %copy-start.1 = (f32[16,32,768]{2,1,0:T(8,128)S(1)}, f32[16,32,768]{2,1,0:T(8,128)}, u32[]{:S(2)}) copy-start(f32[16,32,768]{2,1,0:T(8,128)} %broadcast_add_fusion) | copy-start | bytes 4718596
  165.7 1.4 copy-start
Sparse Core Ops, SparseCore 0:
  31.0 31.6 all-gather.3
  64.3 65.7 all-gather.5
  165.8 64.6 reduce-scatter.1

commit v2 on v0

--- a/solution.py
+++ b/solution.py
@@ -52,7 +52,7 @@
     targets = jnp.arange(QUERIES, dtype=jnp.int32)
     onehot = (queries[:, None] == targets[None, :]).astype(jnp.float32)
     partial_scores = jnp.sum(values[:, None] * onehot, axis=0)
-    scores = lax.psum(partial_scores, ("expert", "matrix"))
+    scores = jnp.sum(lax.all_gather(partial_scores, ("expert", "matrix")), axis=0)
     return (precond[None], scores)
 
 

time: 420 us -> 417 us (level)
    psum x1 -> x0, blocking collectives: 177 us -> none  [shards(): scores = lax.psum(partial_scores, ('expert', 'matrix'))]
    all_gather x0 -> x1, blocking collectives: none -> 174 us  [shards(): lax.all_gather(partial_scores, ('expert', 'matrix'))]
where the time goes in v2:
time: 417 us
  blocking collectives  221 us (53%)
  waiting for transfers between devices  123 us (29%)
  matrix products  35.6 us (9%)
  between operations  15.8 us (4%)
  local copies, waits for them, and re-layouts  12.9 us (3%)
  starting transfers between devices  4.66 us (1%)
  other arithmetic  4.42 us (1%)
    all_gather x1, blocking collectives, shards(): lax.all_gather(partial_scores, ('expert', 'matrix'))  174 us
    reduce_scatter x1, waiting for transfers between devices, shards(): lax.psum_scatter(project_one(jnp.int32(0), own_rows * lax.axis_size('matr...  61.7 us
    all_to_all x1, waiting for transfers between devices, shards(): lax.all_to_all(basis_out, 'expert', split_axis=0, concat_axis=2, tiled=True)  51.2 us
    all_to_all x1, blocking collectives, shards(): lax.all_to_all(eigvals, 'expert', split_axis=0, concat_axis=1, tiled=True)  25.2 us
    all_to_all x1, blocking collectives, shards(): lax.all_to_all(basis_in, 'expert', split_axis=0, concat_axis=1, tiled=True)  21.3 us
    dot_general x1, matrix products, project_one(): return jnp.dot(columns, back, precision=highest)  14.2 us
    dot_general x1, matrix products, shards(): jnp.einsum('ik,if->kf', columns, lax.all_gather(local_rows[0], 'matrix',...  13.4 us
    all_gather x1, waiting for transfers between devices, shards(): lax.all_gather(local_rows[0], 'matrix', axis=0, tiled=True)  9.16 us
  transfers between devices with their start and end apart: 4, of which 3 were waited for; matrix products, arithmetic and copies ran while one was open for 2% of the time, Pallas kernels for 0%

profile of v2, /device:TPU:0, one launch (start us, length us, event | category | flops | bytes accessed | tf_op | source)
XLA Modules:
  0.0 417.0 jit_solution(9197636823018354797)
XLA Ops:
  7.2 0.0 all-gather.5.cloned.1.call-start
  7.2 1.4 copy.14
  8.6 21.3 %all_to_all.36 = f32[16,12,768]{2,1,0:T(8,128)S(1)} all-to-all(f32[16,12,768]{2,1,0:T(8,128)S(1)} %copy.14), channel_id=1, replica_groups=mesh['layer'=2,'expert'=16,'matrix'=4] {'expert'}, dimensions={0} | all-to-all | bytes 1179648 | tf_op jit(solution)/shard_map/all_to_all | solution.py:19
  29.9 0.0 copy-start.2
  29.9 0.9 all_to_all.31
  30.9 0.0 all-gather.5.cloned.1.call-update
  30.9 0.0 all-gather.7.cloned.1.call-start
  30.9 0.7 all-gather.7.cloned.1.call-update
  31.6 0.0 copy-done.2
  31.6 25.2 %all_to_all.37 = f32[16,32,768]{2,1,0:T(8,128)S(1)} all-to-all(f32[16,32,768]{2,1,0:T(8,128)S(1)} %copy-done.2), channel_id=1, replica_groups=mesh['layer'=2,'expert'=16,'matrix'=4] {'expert'}, dimensions={0} | all-to-all | bytes 3145728 | tf_op jit(solution)/shard_map/all_to_all | solution.py:18
  56.8 4.5 %all-to-all-start = ((f32[16,2048,32]{1,2,0:T(8,128)}), f32[16,2048,32]{1,2,0:T(8,128)}, u32[]{:S(2)}, u32[]{:S(2)}) async-start(f32[16,2048,32]{1,2,0:T(8,128)} %param.7), calls=%async_computation | async-start | bytes 8388608 | tf_op jit(solution)/shard_map/all_to_all | solution.py:16
  61.3 0.0 reduce-scatter.2.cloned.1.call-start
  61.4 1.3 broadcast_add_fusion
  62.7 0.0 all-gather.5.cloned.1.call-done
  62.7 2.4 reshape_squeeze.3
  65.1 2.0 copy.15
  67.2 2.6 reshape.43
  69.8 51.2 %all-to-all-done = f32[16,2048,32]{1,2,0:T(8,128)} async-done(((f32[16,2048,32]{1,2,0:T(8,128)}), f32[16,2048,32]{1,2,0:T(8,128)}, u32[]{:S(2)}, u32[]{:S(2)}) %all-to-all-start) | async-done | bytes 4194336 | tf_op jit(solution)/shard_map/all_to_all | solution.py:16
  121.0 9.2 %all-gather.7.cloned.1.call-done = f32[1,1,2048,768]{3,2,1,0:T(8,128)} async-done(((f32[1,1,512,768]{3,2,1,0:T(8,128)}), f32[1,1,2048,768]{3,2,1,0:T(8,128)}) %all-gather.7.cloned.1.call-update) | async-done | bytes 6291472 | tf_op jit(solution)/shard_map/all_gather | solution.py:33
  130.1 0.0 copy-start.1
  130.1 13.4 %fusion = f32[512,768]{1,0:T(8,128)S(1)} fusion(f32[2048,512]{0,1:T(8,128)} %bitcast.2, f32[1,1,2048,768]{3,2,1,0:T(8,128)} %all-gather.7.cloned.1.call-done), kind=kOutput, calls=%fused_computation | convolution fusion | flops 9663676416 | bytes 12058624 | tf_op jit(solution)/shard_map/ik,if->kf/dot_general | solution.py:30
  143.5 0.0 copy-done.1
  143.5 4.1 bitcast_divide_fusion
  147.6 4.0 fusion.4
  151.6 14.2 %convolution_bitcast_fusion = f32[2048,768]{0,1:T(8,128)} fusion(f32[512,768]{1,0:T(8,128)S(1)} %fusion.4, f32[2048,512]{0,1:T(8,128)} %bitcast.2), kind=kOutput, calls=%fused_computation.2 | convolution fusion | flops 9663676416 | bytes 12058624 | tf_op jit(solution)/shard_map/dot_general | solution.py:41
  165.8 0.0 copy-start
  165.8 0.0 reduce-scatter.2.cloned.1.call-update
  165.8 1.4 copy-done
  167.2 0.5 copy.16
  168.9 61.7 %reduce-scatter.2.cloned.1.call-done = f32[512,768]{0,1:T(8,128)} async-done(((f32[2048,768]{0,1:T(8,128)}), f32[512,768]{0,1:T(8,128)}) %reduce-scatter.2.cloned.1.call-update) | async-done | bytes 1572880 | tf_op jit(solution)/shard_map/reduce_scatter | solution.py:43
  230.6 2.5 fusion.2
  233.1 1.6 copy.17
  235.5 174.4 %all-gather.1 = f32[64,1,32]{2,1,0:T(1,128)S(1)} all-gather(f32[1,1,32]{2,1,0:T(1,128)S(1)} %fusion.3), channel_id=1, replica_groups=mesh['layer'=2,'expert'=16,'matrix'=4] {'expert','matrix'}, dimensions={0}, use_global_device_ids=true | all-gather | bytes 8320 | tf_op jit(solution)/shard_map/all_gather | solution.py:55
  409.8 0.6 reduce_sum.20
  (1 shorter events, 0.0 us)
Async XLA Ops:
  7.2 55.5 %all-gather.5.cloned.1.call-start = ((), (), s32[]{:S(2)}) async-start(), calls=%async_computation.4 | async-start | bytes 2949120 | tf_op jit(solution)/shard_map/all_gather | solution.py:21
  29.9 1.7 copy-start.2
  30.9 99.2 %all-gather.7.cloned.1.call-start = ((), (), s32[]{:S(2)}) async-start(), calls=%async_computation.6 | async-start | bytes 7864320 | tf_op jit(solution)/shard_map/all_gather | solution.py:33
  56.8 64.2 %all-to-all-start = ((f32[16,2048,32]{1,2,0:T(8,128)}), f32[16,2048,32]{1,2,0:T(8,128)}, u32[]{:S(2)}, u32[]{:S(2)}) async-start(f32[16,2048,32]{1,2,0:T(8,128)} %param.7), calls=%async_computation | async-start | bytes 8388608 | tf_op jit(solution)/shard_map/all_to_all | solution.py:16
  61.3 169.3 %reduce-scatter.2.cloned.1.call-start = ((), (), s32[]{:S(2)}) async-start(), calls=%async_computation.5 | async-start | bytes 7864320 | tf_op jit(solution)/shard_map/reduce_scatter | solution.py:43
  130.1 13.4 %copy-start.1 = (f32[16,32,768]{2,1,0:T(8,128)S(1)}, f32[16,32,768]{2,1,0:T(8,128)}, u32[]{:S(2)}) copy-start(f32[16,32,768]{2,1,0:T(8,128)} %broadcast_add_fusion) | copy-start | bytes 4718596
  165.8 1.4 copy-start
Sparse Core Ops, SparseCore 0:
  31.0 31.6 all-gather.4
  64.3 65.7 all-gather.6
  165.9 64.6 reduce-scatter.1
